TPU v7x, 128 devices: a whole 4x4x4 slice. The times are simulated.
128 devices in a mesh: bond: 32 (over x, z_lo, y), outer: 4 (over z_hi, core).
Axes of the slice: x: 4, y: 4, z: 4 (z_hi: 2, z_lo: 2; z = z_hi * 2 + z_lo), core: 2. Of those that a mesh axis runs over, the one named last changes fastest.
Arguments:
- upper: bfloat16 [128, 128, 128], P(None, 'bond'), may hold values from -4 to 4
- lower: bfloat16 [128, 128, 8, 128], P(None, 'bond', 'outer'), may hold values from -4 to 4
- isometry: bfloat16 [16384, 128], P(('bond', 'outer')), may hold values from -0.046875 to 0.046875
Outputs:
- coarse: float32 [128, 8, 128], P('bond', 'outer')
All inputs are finite; a program needn't handle non-finite values.
Results may differ from a plain program's by a relative error of at most 0.004.
Values may be sent and summed in bfloat16 or wider, within the bound.
No kernel may reach another device: no remote copies, remote signals or barrier semaphores. Data moves between devices by JAX's collectives and lax.ppermute only.
A program may use at most 64 MiB of HBM per device.

v0:
```python
import jax
import jax.numpy as jnp
from jax import lax
from jax.sharding import PartitionSpec as P


def from_everyone(value, axis):
    peers = lax.axis_size(axis)
    return lax.all_to_all(
        jnp.broadcast_to(value[None], (peers, *value.shape)), axis, 0, 0, tiled=True
    )


def laid_out(tiles, dim):
    dims = list(tiles.shape[1:])
    dims[dim] *= tiles.shape[0]
    return jnp.moveaxis(tiles, 0, dim).reshape(dims)


def gathered_copies(value, axis, dim):
    tiles = from_everyone(value, axis)
    return laid_out(tiles, dim)


def side_by_side(arrays, axis, split_dim, concat_dim, along):
    columns = [a.reshape(*a.shape[:along], -1) for a in arrays]
    both = jnp.concatenate(columns, axis=along)
    whole, at, gathered = (
        lax.all_to_all(both, axis, split_axis=split_dim, concat_axis=concat_dim, tiled=True),
        0,
        [],
    )
    for a, column in zip(arrays, columns):
        slab = whole[..., at : at + column.shape[along]]
        gathered.append(slab.reshape(*slab.shape[:along], *a.shape[along:]))
        at += column.shape[along]
    return tuple(gathered)


def split_up(value, dim, peers):
    before, after = (value.shape[:dim], value.shape[dim + 1 :])
    return jnp.moveaxis(value.reshape(*before, peers, -1, *after), dim, 0)


def sum_at_owner(value, axis, dim):
    peers = lax.axis_size(axis)
    tiles = lax.all_to_all(split_up(value, dim, peers), axis, 0, 0, tiled=True)
    return jnp.sum(tiles, axis=0)


def on_device(upper, lower, isometry):
    grouped = gathered_copies(isometry, "outer", 0)
    gathered = lax.all_gather(grouped, "bond", axis=0, tiled=True)
    upper_local, lower_local = side_by_side((upper, lower), "bond", 0, 1, 2)
    width = gathered.shape[1]
    iso_full = gathered.reshape(width, width, width)
    members = upper_local.shape[0]
    lower_count = lower_local.shape[2]
    own_rows = width // lax.axis_size("bond")

    def member(index, total):
        upper_slab = lax.dynamic_index_in_dim(upper_local, index, 0, keepdims=False)
        lower_slab = lax.dynamic_index_in_dim(lower_local, index, 0, keepdims=False)
        joined = jnp.einsum(
            "lr,lkx->rkx", upper_slab, iso_full, preferred_element_type=jnp.float32
        ).astype(jnp.bfloat16)
        paired = jnp.einsum(
            "rkx,kds->drxs", joined, lower_slab, preferred_element_type=jnp.float32
        ).astype(jnp.bfloat16)
        return total + jnp.einsum(
            "drxs,rsy->xdy", paired, iso_full, preferred_element_type=jnp.float32
        )

    start_total = jnp.zeros((own_rows * lax.axis_size("bond"), lower_count, width), jnp.float32)
    return sum_at_owner(lax.fori_loop(0, members, member, start_total), "bond", 0)


def solution(mesh):
    return jax.shard_map(
        on_device,
        mesh=mesh,
        in_specs=(
            P(None, "bond", None),
            P(None, "bond", "outer", None),
            P(("bond", "outer"), None),
        ),
        out_specs=P("bond", "outer", None),
        check_vma=False,
    )
```

profile of v0, /device:TPU:0, one launch (start us, length us, event | category | flops | bytes accessed | tf_op | source)
XLA Modules:
  0.0 266.1 jit_solution(133806632198661356)
XLA Ops:
  6.5 0.0 all-gather.2.cloned.1.call-start
  6.5 0.8 broadcast_in_dim.10
  7.3 11.3 %all_to_all.28 = bf16[4,128,128]{2,1,0:T(8,128)(2,1)} all-to-all(bf16[4,128,128]{2,1,0:T(8,128)(2,1)S(1)} %broadcast_in_dim.10), channel_id=1, replica_groups=mesh['bond'=32,'outer'=4] {'outer'}, dimensions={0} | all-to-all | bytes 262144 | tf_op jit(solution)/shard_map/all_to_all | solution.py:9
  18.6 0.0 all-gather.2.cloned.1.call-update
  18.6 1.1 reshape.16
  19.7 1.8 pad_maximum_fusion
  21.6 7.8 %all-to-all-start = ((bf16[128,4,384]{2,1,0:T(4,128)(2,1)}), bf16[128,4,384]{2,1,0:T(4,128)(2,1)S(1)}, u32[]{:S(2)}, u32[]{:S(2)}) async-start(bf16[128,4,384]{2,1,0:T(4,128)(2,1)} %pad_maximum_fusion), calls=%async_computation | async-start | bytes 786432 | tf_op jit(solution)/shard_map/all_to_all | solution.py:29
  29.4 10.5 %all-to-all-done = bf16[128,4,384]{2,1,0:T(4,128)(2,1)S(1)} async-done(((bf16[128,4,384]{2,1,0:T(4,128)(2,1)}), bf16[128,4,384]{2,1,0:T(4,128)(2,1)S(1)}, u32[]{:S(2)}, u32[]{:S(2)}) %all-to-all-start) | async-done | bytes 393248 | tf_op jit(solution)/shard_map/all_to_all | solution.py:29
  39.9 0.2 copy.21
  40.0 0.1 slice.8
  40.2 0.2 copy.30
  40.4 0.1 copy.23
  40.6 135.7 %all-gather.2.cloned.1.call-done = bf16[16384,128]{1,0:T(8,128)(2,1)} async-done(((bf16[512,128]{1,0:T(8,128)(2,1)}), bf16[16384,128]{1,0:T(8,128)(2,1)}) %all-gather.2.cloned.1.call-update) | async-done | bytes 4194320 | tf_op jit(solution)/shard_map/all_gather | solution.py:53
  176.3 67.8 %while.14 = (s32[]{:T(128)}, f32[128,2,128]{2,0,1:T(8,128)S(1)}, bf16[4,128,2,128]{1,3,2,0:T(8,128)(2,1)S(1)}, bf16[4,128,128]{1,2,0:T(8,128)(2,1)S(1)}, bf16[12...) while((s32[]{:T(128)}, f32[128,2,128]{2,0,1:T(8,128)S(1)}, ...), condition=%wide.region_1.2_spmd.clone, body=%wide.region_0.1_spmd.clone.sunk | while | flops 2690711552 | bytes 17137760 | solution.py:75
  176.3 7.5 %fusion.52 = bf16[128,128,128]{2,0,1:T(8,128)(2,1)} fusion(bf16[128,128,128]{2,1,0:T(8,128)(2,1)} %get-tuple-element.192, bf16[4,128,128]{1,2,0:T(8,128)(2,1)S(1)} %get-tuple-element.191, s32[]{:T(128)} %get-tuple-element.181), kind=kOutput, calls=%fused_computation.9.clone.1 | convolution fusion | flops 538968064 | bytes 8421380 | tf_op jit(solution)/shard_map/while/body/eval_jaxpr/lr,lkx->rkx/dot_general | solution.py:64
  183.8 9.4 %fusion.53 = f32[128,2,128]{2,0,1:T(8,128)S(1)} fusion(bf16[128,128,128]{2,1,0:T(8,128)(2,1)} %get-tuple-element.192, bf16[128,128,128]{2,0,1:T(8,128)(2,1)} %fusion.52, f32[128,2,128]{2,0,1:T(8,128)S(1)} %get-tuple-element.182, bf16[4,128,2,128]{1,3,2,0:T(8,128)(2,1)S(1)} %get-tuple-element.190, s32[]{:T(128)} %get-tuple-element.181, pred[]{:T(512)S(6)} %compare.3), kind=kOutput, calls=%fused_computation.11.clone.1 | convolution fusion | flops 2151743488 | bytes 8716293 | tf_op jit(solution)/shard_map/while/body/eval_jaxpr/drxs,rsy->xdy/dot_general | solution.py:70
  193.3 7.5 %fusion.52 = bf16[128,128,128]{2,0,1:T(8,128)(2,1)} fusion(bf16[128,128,128]{2,1,0:T(8,128)(2,1)} %get-tuple-element.192, bf16[4,128,128]{1,2,0:T(8,128)(2,1)S(1)} %get-tuple-element.191, s32[]{:T(128)} %get-tuple-element.181), kind=kOutput, calls=%fused_computation.9.clone.1 | convolution fusion | flops 538968064 | bytes 8421380 | tf_op jit(solution)/shard_map/while/body/eval_jaxpr/lr,lkx->rkx/dot_general | solution.py:64
  200.8 9.4 %fusion.53 = f32[128,2,128]{2,0,1:T(8,128)S(1)} fusion(bf16[128,128,128]{2,1,0:T(8,128)(2,1)} %get-tuple-element.192, bf16[128,128,128]{2,0,1:T(8,128)(2,1)} %fusion.52, f32[128,2,128]{2,0,1:T(8,128)S(1)} %get-tuple-element.182, bf16[4,128,2,128]{1,3,2,0:T(8,128)(2,1)S(1)} %get-tuple-element.190, s32[]{:T(128)} %get-tuple-element.181, pred[]{:T(512)S(6)} %compare.3), kind=kOutput, calls=%fused_computation.11.clone.1 | convolution fusion | flops 2151743488 | bytes 8716293 | tf_op jit(solution)/shard_map/while/body/eval_jaxpr/drxs,rsy->xdy/dot_general | solution.py:70
  210.2 7.5 %fusion.52 = bf16[128,128,128]{2,0,1:T(8,128)(2,1)} fusion(bf16[128,128,128]{2,1,0:T(8,128)(2,1)} %get-tuple-element.192, bf16[4,128,128]{1,2,0:T(8,128)(2,1)S(1)} %get-tuple-element.191, s32[]{:T(128)} %get-tuple-element.181), kind=kOutput, calls=%fused_computation.9.clone.1 | convolution fusion | flops 538968064 | bytes 8421380 | tf_op jit(solution)/shard_map/while/body/eval_jaxpr/lr,lkx->rkx/dot_general | solution.py:64
  217.7 9.4 %fusion.53 = f32[128,2,128]{2,0,1:T(8,128)S(1)} fusion(bf16[128,128,128]{2,1,0:T(8,128)(2,1)} %get-tuple-element.192, bf16[128,128,128]{2,0,1:T(8,128)(2,1)} %fusion.52, f32[128,2,128]{2,0,1:T(8,128)S(1)} %get-tuple-element.182, bf16[4,128,2,128]{1,3,2,0:T(8,128)(2,1)S(1)} %get-tuple-element.190, s32[]{:T(128)} %get-tuple-element.181, pred[]{:T(512)S(6)} %compare.3), kind=kOutput, calls=%fused_computation.11.clone.1 | convolution fusion | flops 2151743488 | bytes 8716293 | tf_op jit(solution)/shard_map/while/body/eval_jaxpr/drxs,rsy->xdy/dot_general | solution.py:70
  227.1 7.5 %fusion.52 = bf16[128,128,128]{2,0,1:T(8,128)(2,1)} fusion(bf16[128,128,128]{2,1,0:T(8,128)(2,1)} %get-tuple-element.192, bf16[4,128,128]{1,2,0:T(8,128)(2,1)S(1)} %get-tuple-element.191, s32[]{:T(128)} %get-tuple-element.181), kind=kOutput, calls=%fused_computation.9.clone.1 | convolution fusion | flops 538968064 | bytes 8421380 | tf_op jit(solution)/shard_map/while/body/eval_jaxpr/lr,lkx->rkx/dot_general | solution.py:64
  234.7 9.4 %fusion.53 = f32[128,2,128]{2,0,1:T(8,128)S(1)} fusion(bf16[128,128,128]{2,1,0:T(8,128)(2,1)} %get-tuple-element.192, bf16[128,128,128]{2,0,1:T(8,128)(2,1)} %fusion.52, f32[128,2,128]{2,0,1:T(8,128)S(1)} %get-tuple-element.182, bf16[4,128,2,128]{1,3,2,0:T(8,128)(2,1)S(1)} %get-tuple-element.190, s32[]{:T(128)} %get-tuple-element.181, pred[]{:T(512)S(6)} %compare.3), kind=kOutput, calls=%fused_computation.11.clone.1 | convolution fusion | flops 2151743488 | bytes 8716293 | tf_op jit(solution)/shard_map/while/body/eval_jaxpr/drxs,rsy->xdy/dot_general | solution.py:70
  244.1 14.5 %all_to_all.29 = f32[32,4,2,128]{3,1,2,0:T(4,128)S(1)} all-to-all(f32[32,4,2,128]{3,1,2,0:T(4,128)S(1)} %copy.24), channel_id=1, replica_groups=mesh['bond'=32,'outer'=4] {'bond'}, dimensions={0} | all-to-all | bytes 262144 | tf_op jit(solution)/shard_map/all_to_all | solution.py:47
  258.7 0.6 copy.26
  (4 shorter events, 0.1 us)
Async XLA Ops:
  6.5 169.8 %all-gather.2.cloned.1.call-start = ((), (), s32[]{:S(2)}) async-start(), calls=%async_computation.3 | async-start | bytes 4325376 | tf_op jit(solution)/shard_map/all_gather | solution.py:53
  21.6 18.3 %all-to-all-start = ((bf16[128,4,384]{2,1,0:T(4,128)(2,1)}), bf16[128,4,384]{2,1,0:T(4,128)(2,1)S(1)}, u32[]{:S(2)}, u32[]{:S(2)}) async-start(bf16[128,4,384]{2,1,0:T(4,128)(2,1)} %pad_maximum_fusion), calls=%async_computation | async-start | bytes 786432 | tf_op jit(solution)/shard_map/all_to_all | solution.py:29
Sparse Core Ops, SparseCore 0:
  18.7 157.5 all-gather.1
where the time goes:
time: 267 us; the launch traced here: 266 us
  waiting for transfers between devices  146 us (55%)
  matrix products  67.7 us (25%)
  blocking collectives  25.8 us (10%)
  between operations  13.5 us (5%)
  starting transfers between devices  7.78 us (3%)
  local copies, waits for them, and re-layouts  3.18 us (1%)
    all_gather x1, waiting for transfers between devices, on_device(): gathered = lax.all_gather(grouped, 'bond', axis=0, tiled=True)  136 us
    dot_general x4, matrix products, member(): jnp.einsum('drxs,rsy->xdy', paired, iso_full, preferred_element_type=jnp....  37.5 us
    dot_general x4, matrix products, member(): jnp.einsum('lr,lkx->rkx', upper_slab, iso_full, preferred_element_type=jn...  30.1 us
    all_to_all x1, blocking collectives, sum_at_owner(): tiles = lax.all_to_all(split_up(value, dim, peers), axis, 0, 0, tiled=True)  14.5 us
    all_to_all x1, blocking collectives, from_everyone(): lax.all_to_all(jnp.broadcast_to(value[None], (peers, *value.shape)), axis...  11.3 us
    all_to_all x1, waiting for transfers between devices, side_by_side(): lax.all_to_all(both, axis, split_axis=split_dim, concat_axis=concat_dim,...  10.5 us
    all_to_all x1, starting transfers between devices, side_by_side(): lax.all_to_all(both, axis, split_axis=split_dim, concat_axis=concat_dim,...  7.77 us
  transfers between devices with their start and end apart: 2, of which 2 were waited for; matrix products, arithmetic and copies ran while one was open for 1% of the time, Pallas kernels for 0%

commit v1 on v0

--- a/solution.py
+++ b/solution.py
@@ -50,7 +50,9 @@
 
 def on_device(upper, lower, isometry):
     grouped = gathered_copies(isometry, "outer", 0)
-    gathered = lax.all_gather(grouped, "bond", axis=0, tiled=True)
+    gathered = jnp.concatenate(
+        lax.all_to_all(jnp.stack([grouped] * lax.axis_size("bond")), "bond", 0, 0), axis=0
+    )
     upper_local, lower_local = side_by_side((upper, lower), "bond", 0, 1, 2)
     width = gathered.shape[1]
     iso_full = gathered.reshape(width, width, width)

time: 267 us -> 179 us (0.67)
  waiting for transfers between devices: 146 us -> 60.7 us
  between operations: 13.5 us -> 0.08 us
  blocking collectives: 25.8 us -> 31.9 us
  local copies, waits for them, and re-layouts: 3.18 us -> 6.74 us
    all_gather x1 -> x0, waiting for transfers between devices: 136 us -> none  [on_device(): gathered = lax.all_gather(grouped, 'bond', axis=0, tiled=True)]
    all_to_all x1 -> x2, waiting for transfers between devices: 10.5 us -> 60.7 us  [the longest x1 56.8 us: on_device(): lax.all_to_all(jnp.stack([grouped] * lax.axis_size('bond')), 'bond', 0, 0)]
    all_to_all x1, blocking collectives: 11.3 us -> 17.7 us  [side_by_side(): lax.all_to_all(both, axis, split_axis=split_dim, concat_axis=concat_dim,...]
    another operation x0 -> x1, local copies, waits for them, and re-layouts: none -> 2.92 us  [on_device(): jnp.stack([grouped] * lax.axis_size('bond'))]
    all_to_all x1 -> x2, starting transfers between devices: 7.77 us -> 10.1 us  [the longest x1 5.26 us: from_everyone(): lax.all_to_all(jnp.broadcast_to(value[None], (peers, *value.shape)), axis...]
  transfers between devices with their start and end apart: 2 -> 2, of which waited for: 2 -> 2; matrix products, arithmetic and copies ran while one was open for 1% -> 2% of each run, Pallas kernels for 0% -> 0%
where the time goes in v1:
time: 179 us; the launch traced here: 178 us
  matrix products  67.7 us (38%)
  waiting for transfers between devices  60.7 us (34%)
  blocking collectives  31.9 us (18%)
  starting transfers between devices  10.1 us (6%)
  local copies, waits for them, and re-layouts  6.74 us (4%)
    all_to_all x1, waiting for transfers between devices, on_device(): lax.all_to_all(jnp.stack([grouped] * lax.axis_size('bond')), 'bond', 0, 0)  56.8 us
    dot_general x4, matrix products, member(): jnp.einsum('drxs,rsy->xdy', paired, iso_full, preferred_element_type=jnp....  37.5 us
    dot_general x4, matrix products, member(): jnp.einsum('lr,lkx->rkx', upper_slab, iso_full, preferred_element_type=jn...  30.2 us
    all_to_all x1, blocking collectives, side_by_side(): lax.all_to_all(both, axis, split_axis=split_dim, concat_axis=concat_dim,...  17.7 us
    all_to_all x1, blocking collectives, sum_at_owner(): tiles = lax.all_to_all(split_up(value, dim, peers), axis, 0, 0, tiled=True)  14.2 us
    all_to_all x1, starting transfers between devices, from_everyone(): lax.all_to_all(jnp.broadcast_to(value[None], (peers, *value.shape)), axis...  5.26 us
    all_to_all x1, starting transfers between devices, on_device(): lax.all_to_all(jnp.stack([grouped] * lax.axis_size('bond')), 'bond', 0, 0)  4.86 us
    all_to_all x1, waiting for transfers between devices, from_everyone(): lax.all_to_all(jnp.broadcast_to(value[None], (peers, *value.shape)), axis...  3.9 us
  transfers between devices with their start and end apart: 2, of which 2 were waited for; matrix products, arithmetic and copies ran while one was open for 2% of the time, Pallas kernels for 0%

profile of v1, /device:TPU:0, one launch (start us, length us, event | category | flops | bytes accessed | tf_op | source)
XLA Modules:
  0.0 178.4 jit_solution(13680053936250075184)
XLA Ops:
  0.0 1.4 broadcast_in_dim.10
  1.4 5.3 %all-to-all-start.1 = ((bf16[4,128,128]{2,1,0:T(8,128)(2,1)}), bf16[4,128,128]{2,1,0:T(8,128)(2,1)S(1)}, u32[]{:S(2)}, u32[]{:S(2)}) async-start(bf16[4,128,128]{2,1,0:T(8,128)(2,1)} %broadcast_in_dim.10), calls=%async_computation.1 | async-start | bytes 262144 | tf_op jit(solution)/shard_map/all_to_all | solution.py:9
  6.7 1.1 reshape.12
  7.8 1.1 pad_maximum_fusion
  8.9 3.9 %all-to-all-done.1 = bf16[4,128,128]{2,1,0:T(8,128)(2,1)S(1)} async-done(((bf16[4,128,128]{2,1,0:T(8,128)(2,1)}), bf16[4,128,128]{2,1,0:T(8,128)(2,1)S(1)}, u32[]{:S(2)}, u32[]{:S(2)}) %all-to-all-start.1) | async-done | bytes 131104 | tf_op jit(solution)/shard_map/all_to_all | solution.py:9
  12.8 17.7 %all_to_all.33 = bf16[128,4,384]{2,1,0:T(4,128)(2,1)S(1)} all-to-all(bf16[128,4,384]{2,1,0:T(4,128)(2,1)S(1)} %pad_maximum_fusion), channel_id=1, replica_groups=mesh['bond'=32,'outer'=4] {'bond'}, dimensions={0} | all-to-all | bytes 786432 | tf_op jit(solution)/shard_map/all_to_all | solution.py:29
  30.5 2.9 %stack.3 = bf16[32,512,128]{2,1,0:T(8,128)(2,1)} broadcast(bf16[512,128]{1,0:T(8,128)(2,1)S(1)} %bitcast.63), dimensions={1,2} | broadcast | bytes 4325376 | tf_op jit(solution)/shard_map/stack | solution.py:54
  33.4 4.9 %all-to-all-start.2 = ((bf16[32,512,128]{2,1,0:T(8,128)(2,1)}), bf16[32,512,128]{2,1,0:T(8,128)(2,1)}, u32[]{:S(2)}, u32[]{:S(2)}) async-start(bf16[32,512,128]{2,1,0:T(8,128)(2,1)} %stack.3), calls=%async_computation.2 | async-start | bytes 8388608 | tf_op jit(solution)/shard_map/all_to_all | solution.py:54
  38.3 0.2 copy.21
  38.5 0.1 slice.8
  38.6 0.2 copy.30
  38.8 0.1 copy.23
  39.0 56.8 %all-to-all-done.2 = bf16[32,512,128]{2,1,0:T(8,128)(2,1)} async-done(((bf16[32,512,128]{2,1,0:T(8,128)(2,1)}), bf16[32,512,128]{2,1,0:T(8,128)(2,1)}, u32[]{:S(2)}, u32[]{:S(2)}) %all-to-all-start.2) | async-done | bytes 4194336 | tf_op jit(solution)/shard_map/all_to_all | solution.py:54
  95.8 67.8 %while.14 = (s32[]{:T(128)}, f32[128,2,128]{2,0,1:T(8,128)S(1)}, bf16[4,128,2,128]{1,3,2,0:T(8,128)(2,1)S(1)}, bf16[4,128,128]{1,2,0:T(8,128)(2,1)S(1)}, bf16[12...) while((s32[]{:T(128)}, f32[128,2,128]{2,0,1:T(8,128)S(1)}, ...), condition=%wide.region_1.2_spmd.clone, body=%wide.region_0.1_spmd.clone.sunk | while | flops 2690711552 | bytes 17137760 | solution.py:77
  95.8 7.5 %fusion.52 = bf16[128,128,128]{2,0,1:T(8,128)(2,1)} fusion(bf16[128,128,128]{2,1,0:T(8,128)(2,1)} %get-tuple-element.192, bf16[4,128,128]{1,2,0:T(8,128)(2,1)S(1)} %get-tuple-element.191, s32[]{:T(128)} %get-tuple-element.181), kind=kOutput, calls=%fused_computation.9.clone.1 | convolution fusion | flops 538968064 | bytes 8421380 | tf_op jit(solution)/shard_map/while/body/eval_jaxpr/lr,lkx->rkx/dot_general | solution.py:66
  103.3 9.4 %fusion.53 = f32[128,2,128]{2,0,1:T(8,128)S(1)} fusion(bf16[128,128,128]{2,1,0:T(8,128)(2,1)} %get-tuple-element.192, bf16[128,128,128]{2,0,1:T(8,128)(2,1)} %fusion.52, f32[128,2,128]{2,0,1:T(8,128)S(1)} %get-tuple-element.182, bf16[4,128,2,128]{1,3,2,0:T(8,128)(2,1)S(1)} %get-tuple-element.190, s32[]{:T(128)} %get-tuple-element.181, pred[]{:T(512)S(6)} %compare.3), kind=kOutput, calls=%fused_computation.11.clone.1 | convolution fusion | flops 2151743488 | bytes 8716293 | tf_op jit(solution)/shard_map/while/body/eval_jaxpr/drxs,rsy->xdy/dot_general | solution.py:72
  112.7 7.5 %fusion.52 = bf16[128,128,128]{2,0,1:T(8,128)(2,1)} fusion(bf16[128,128,128]{2,1,0:T(8,128)(2,1)} %get-tuple-element.192, bf16[4,128,128]{1,2,0:T(8,128)(2,1)S(1)} %get-tuple-element.191, s32[]{:T(128)} %get-tuple-element.181), kind=kOutput, calls=%fused_computation.9.clone.1 | convolution fusion | flops 538968064 | bytes 8421380 | tf_op jit(solution)/shard_map/while/body/eval_jaxpr/lr,lkx->rkx/dot_general | solution.py:66
  120.3 9.4 %fusion.53 = f32[128,2,128]{2,0,1:T(8,128)S(1)} fusion(bf16[128,128,128]{2,1,0:T(8,128)(2,1)} %get-tuple-element.192, bf16[128,128,128]{2,0,1:T(8,128)(2,1)} %fusion.52, f32[128,2,128]{2,0,1:T(8,128)S(1)} %get-tuple-element.182, bf16[4,128,2,128]{1,3,2,0:T(8,128)(2,1)S(1)} %get-tuple-element.190, s32[]{:T(128)} %get-tuple-element.181, pred[]{:T(512)S(6)} %compare.3), kind=kOutput, calls=%fused_computation.11.clone.1 | convolution fusion | flops 2151743488 | bytes 8716293 | tf_op jit(solution)/shard_map/while/body/eval_jaxpr/drxs,rsy->xdy/dot_general | solution.py:72
  129.7 7.5 %fusion.52 = bf16[128,128,128]{2,0,1:T(8,128)(2,1)} fusion(bf16[128,128,128]{2,1,0:T(8,128)(2,1)} %get-tuple-element.192, bf16[4,128,128]{1,2,0:T(8,128)(2,1)S(1)} %get-tuple-element.191, s32[]{:T(128)} %get-tuple-element.181), kind=kOutput, calls=%fused_computation.9.clone.1 | convolution fusion | flops 538968064 | bytes 8421380 | tf_op jit(solution)/shard_map/while/body/eval_jaxpr/lr,lkx->rkx/dot_general | solution.py:66
  137.2 9.4 %fusion.53 = f32[128,2,128]{2,0,1:T(8,128)S(1)} fusion(bf16[128,128,128]{2,1,0:T(8,128)(2,1)} %get-tuple-element.192, bf16[128,128,128]{2,0,1:T(8,128)(2,1)} %fusion.52, f32[128,2,128]{2,0,1:T(8,128)S(1)} %get-tuple-element.182, bf16[4,128,2,128]{1,3,2,0:T(8,128)(2,1)S(1)} %get-tuple-element.190, s32[]{:T(128)} %get-tuple-element.181, pred[]{:T(512)S(6)} %compare.3), kind=kOutput, calls=%fused_computation.11.clone.1 | convolution fusion | flops 2151743488 | bytes 8716293 | tf_op jit(solution)/shard_map/while/body/eval_jaxpr/drxs,rsy->xdy/dot_general | solution.py:72
  146.6 7.5 %fusion.52 = bf16[128,128,128]{2,0,1:T(8,128)(2,1)} fusion(bf16[128,128,128]{2,1,0:T(8,128)(2,1)} %get-tuple-element.192, bf16[4,128,128]{1,2,0:T(8,128)(2,1)S(1)} %get-tuple-element.191, s32[]{:T(128)} %get-tuple-element.181), kind=kOutput, calls=%fused_computation.9.clone.1 | convolution fusion | flops 538968064 | bytes 8421380 | tf_op jit(solution)/shard_map/while/body/eval_jaxpr/lr,lkx->rkx/dot_general | solution.py:66
  154.2 9.4 %fusion.53 = f32[128,2,128]{2,0,1:T(8,128)S(1)} fusion(bf16[128,128,128]{2,1,0:T(8,128)(2,1)} %get-tuple-element.192, bf16[128,128,128]{2,0,1:T(8,128)(2,1)} %fusion.52, f32[128,2,128]{2,0,1:T(8,128)S(1)} %get-tuple-element.182, bf16[4,128,2,128]{1,3,2,0:T(8,128)(2,1)S(1)} %get-tuple-element.190, s32[]{:T(128)} %get-tuple-element.181, pred[]{:T(512)S(6)} %compare.3), kind=kOutput, calls=%fused_computation.11.clone.1 | convolution fusion | flops 2151743488 | bytes 8716293 | tf_op jit(solution)/shard_map/while/body/eval_jaxpr/drxs,rsy->xdy/dot_general | solution.py:72
  163.6 14.2 %all_to_all.34 = f32[32,4,2,128]{3,1,2,0:T(4,128)S(1)} all-to-all(f32[32,4,2,128]{3,1,2,0:T(4,128)S(1)} %copy.24), channel_id=1, replica_groups=mesh['bond'=32,'outer'=4] {'bond'}, dimensions={0} | all-to-all | bytes 262144 | tf_op jit(solution)/shard_map/all_to_all | solution.py:47
  177.8 0.6 copy.26
  (4 shorter events, 0.1 us)
Async XLA Ops:
  1.4 11.4 %all-to-all-start.1 = ((bf16[4,128,128]{2,1,0:T(8,128)(2,1)}), bf16[4,128,128]{2,1,0:T(8,128)(2,1)S(1)}, u32[]{:S(2)}, u32[]{:S(2)}) async-start(bf16[4,128,128]{2,1,0:T(8,128)(2,1)} %broadcast_in_dim.10), calls=%async_computation.1 | async-start | bytes 262144 | tf_op jit(solution)/shard_map/all_to_all | solution.py:9
  33.4 62.4 %all-to-all-start.2 = ((bf16[32,512,128]{2,1,0:T(8,128)(2,1)}), bf16[32,512,128]{2,1,0:T(8,128)(2,1)}, u32[]{:S(2)}, u32[]{:S(2)}) async-start(bf16[32,512,128]{2,1,0:T(8,128)(2,1)} %stack.3), calls=%async_computation.2 | async-start | bytes 8388608 | tf_op jit(solution)/shard_map/all_to_all | solution.py:54
